TPU v7x, 64 devices: a 2x2x8 block of a 4x4x8 slice. The times are simulated.
64 devices in a mesh: rep: 8 (over x, y, core), dp: 8 (over z).
Axes of the slice: x: 2, y: 2, z: 8, core: 2. Of those that a mesh axis runs over, the one named last changes fastest.
The devices are a block of a 4x4x8 slice.
Arguments:
- g_w_gate: bfloat16 [64, 2, 512, 1408], P(('rep', 'dp')), parts along dimension 0
- g_w_up: bfloat16 [64, 2, 512, 1408], P(('rep', 'dp')), parts along dimension 0
- g_w_down: bfloat16 [64, 2, 1408, 512], P(('rep', 'dp')), parts along dimension 0
- w_gate: bfloat16 [2, 512, 1408], replicated
- w_up: bfloat16 [2, 512, 1408], replicated
- w_down: bfloat16 [2, 1408, 512], replicated
- m_w_gate: float32 [2, 512, 1408], P(None, 'dp')
- m_w_up: float32 [2, 512, 1408], P(None, 'dp')
- m_w_down: float32 [2, 1408, 512], P(None, 'dp')
- v_w_gate: float32 [2, 512, 1408], P(None, 'dp')
- v_w_up: float32 [2, 512, 1408], P(None, 'dp')
- v_w_down: float32 [2, 1408, 512], P(None, 'dp')
Outputs:
- output 1: bfloat16 [16, 512, 1408], P('rep'), parts along dimension 0
- output 2: bfloat16 [16, 512, 1408], P('rep'), parts along dimension 0
- output 3: bfloat16 [16, 1408, 512], P('rep'), parts along dimension 0
- output 4: float32 [16, 512, 1408], P('rep', 'dp'), parts along dimension 0
- output 5: float32 [16, 512, 1408], P('rep', 'dp'), parts along dimension 0
- output 6: float32 [16, 1408, 512], P('rep', 'dp'), parts along dimension 0
- output 7: float32 [16, 512, 1408], P('rep', 'dp'), parts along dimension 0
- output 8: float32 [16, 512, 1408], P('rep', 'dp'), parts along dimension 0
- output 9: float32 [16, 1408, 512], P('rep', 'dp'), parts along dimension 0
There are 8 independent parts. A program takes and returns all parts, laid end to end along the dimension named above; an argument that names none is the same for every part.
All inputs are finite; a program needn't handle non-finite values.
Results may differ from a plain program's by a relative error of at most 0.022.
Values are sent between devices in bfloat16 or wider.
A program may use at most 768 MiB of HBM per device.

v0:
```python
import jax
import jax.numpy as jnp
from jax import lax
from jax.sharding import PartitionSpec as P


def adamw(w, m, v, g):
    m = 0.9 * m + 0.1 * g
    v = 0.95 * v + 0.05 * g * g
    step = m * lax.rsqrt(v + 1e-8) + 0.1 * w
    return (w - 0.02 * step).astype(jnp.bfloat16), m, v


def clipped(gradients, sum_of_squares, count):
    factor = jnp.minimum(1.0, 0.5 * lax.rsqrt(sum_of_squares / count + 1e-30))
    return [g * factor for g in gradients]


def solution(mesh):
    def step(*arrays):
        terms, weights, m, v = (arrays[i : i + 3] for i in (0, 3, 6, 9))
        gradients = [lax.psum_scatter(t[0], "dp", scatter_dimension=1, tiled=True).astype(jnp.float32) for t in terms]
        squares = lax.psum(sum(jnp.sum(g * g) for g in gradients), "dp")
        gradients = clipped(gradients, squares, lax.psum(1, "dp") * sum(g.size for g in gradients))
        me = lax.axis_index("dp")
        own = [lax.dynamic_slice_in_dim(w, me * one.shape[1], one.shape[1], 1).astype(jnp.float32) for w, one in zip(weights, m, strict=True)]
        new = [adamw(w, m, v, g) for w, m, v, g in zip(own, m, v, gradients, strict=True)]
        whole = [lax.all_gather(one[0], "dp", axis=1, tiled=True) for one in new]
        return (*whole, *(one[1] for one in new), *(one[2] for one in new))

    all_of, cut = P(None, None, None), P(None, "dp", None)
    return jax.shard_map(
        step,
        mesh=mesh,
        in_specs=(P(("rep", "dp"), None, None, None),) * 3 + (all_of,) * 3 + (cut,) * 6,
        out_specs=(P("rep", None, None),) * 3 + (P("rep", "dp", None),) * 6,
        check_vma=False,
    )
```

profile of v0, /device:TPU:22, one launch (start us, length us, event | category | flops | bytes accessed | tf_op | source)
XLA Modules:
  0.0 302.0 jit_solution(13045758538505573526)
XLA Ops:
  7.2 0.1 reduce-scatter.4.cloned.1.call-start
  7.3 0.7 reduce-scatter.4.cloned.1.call-update
  8.0 0.1 reduce-scatter.6.cloned.1.call-start
  8.1 0.0 copy-start.4
  8.1 0.0 copy-start.5
  8.1 0.7 reduce-scatter.6.cloned.1.call-update
  8.8 0.1 reduce-scatter.8.cloned.1.call-start
  8.9 0.7 reduce-scatter.8.cloned.1.call-update
  9.6 0.0 copy-start.7
  9.6 0.1 all-gather.8.cloned.1.call-start
  9.7 46.4 %reduce-scatter.4.cloned.1.call-done = bf16[2,64,1408]{2,1,0:T(8,128)(2,1)} async-done(((bf16[2,512,1408]{2,1,0:T(8,128)(2,1)}), bf16[2,64,1408]{2,1,0:T(8,128)(2,1)}) %reduce-scatter.4.cloned.1.call-update) | async-done | bytes 360464 | tf_op jit(solution)/shard_map/reduce_scatter | solution.py:22
  56.1 1.8 fusion.9
  58.0 42.1 %reduce-scatter.6.cloned.1.call-done = bf16[2,64,1408]{2,1,0:T(8,128)(2,1)} async-done(((bf16[2,512,1408]{2,1,0:T(8,128)(2,1)}), bf16[2,64,1408]{2,1,0:T(8,128)(2,1)}) %reduce-scatter.6.cloned.1.call-update) | async-done | bytes 360464 | tf_op jit(solution)/shard_map/reduce_scatter | solution.py:22
  100.0 1.8 fusion.10
  103.1 40.9 %reduce-scatter.8.cloned.1.call-done = bf16[2,176,512]{2,1,0:T(8,128)(2,1)} async-done(((bf16[2,1408,512]{2,1,0:T(8,128)(2,1)}), bf16[2,176,512]{2,1,0:T(8,128)(2,1)}) %reduce-scatter.8.cloned.1.call-update) | async-done | bytes 360464 | tf_op jit(solution)/shard_map/reduce_scatter | solution.py:22
  144.0 1.8 fusion.11
  146.4 16.4 %psum.7 = f32[]{:T(128)} all-reduce(f32[]{:T(128)S(6)} %add.65), channel_id=1, replica_groups=mesh['rep'=8,'dp'=8] {'dp'}, use_global_device_ids=true, to_apply=%region_6.0 | all-reduce | flops 1 | bytes 8 | tf_op jit(solution)/shard_map/psum | solution.py:23
  163.5 2.5 fusion.17
  166.0 0.1 all-gather.8.cloned.1.call-update
  166.1 0.1 all-gather.4.cloned.1.call-start
  166.2 2.5 fusion.8
  168.7 0.1 all-gather.4.cloned.1.call-update
  168.7 0.1 all-gather.6.cloned.1.call-start
  168.8 2.6 fusion.14
  171.5 0.1 all-gather.6.cloned.1.call-update
  171.5 34.3 %all-gather.8.cloned.1.call-done = bf16[2,1408,512]{2,1,0:T(8,128)(2,1)} async-done(((bf16[2,176,512]{2,1,0:T(8,128)(2,1)}), bf16[2,1408,512]{2,1,0:T(8,128)(2,1)}) %all-gather.8.cloned.1.call-update) | async-done | bytes 2883600 | tf_op jit(solution)/shard_map/all_gather | solution.py:28
  205.8 40.5 %all-gather.4.cloned.1.call-done = bf16[2,512,1408]{2,1,0:T(8,128)(2,1)} async-done(((bf16[2,64,1408]{2,1,0:T(8,128)(2,1)}), bf16[2,512,1408]{2,1,0:T(8,128)(2,1)}) %all-gather.4.cloned.1.call-update) | async-done | bytes 2883600 | tf_op jit(solution)/shard_map/all_gather | solution.py:28
  246.4 40.6 %all-gather.6.cloned.1.call-done = bf16[2,512,1408]{2,1,0:T(8,128)(2,1)} async-done(((bf16[2,64,1408]{2,1,0:T(8,128)(2,1)}), bf16[2,512,1408]{2,1,0:T(8,128)(2,1)}) %all-gather.6.cloned.1.call-update) | async-done | bytes 2883600 | tf_op jit(solution)/shard_map/all_gather | solution.py:28
  286.9 3.8 %copy.24 = bf16[2,512,1408]{2,1,0:T(8,128)(2,1)} copy(bf16[2,512,1408]{2,1,0:T(8,128)(2,1)} %all-gather.4.cloned.1.call-done) | data formatting | bytes 5767168
  290.7 1.6 copy.25
  292.3 1.3 copy-done
  293.6 1.6 copy.26
  (14 shorter events, 0.0 us)
Async XLA Ops:
  7.2 48.9 %reduce-scatter.4.cloned.1.call-start = ((), (), s32[]{:S(2)}) async-start(), calls=%async_computation.3 | async-start | bytes 3244032 | tf_op jit(solution)/shard_map/reduce_scatter | solution.py:22
  8.0 92.1 %reduce-scatter.6.cloned.1.call-start = ((), (), s32[]{:S(2)}) async-start(), calls=%async_computation.4 | async-start | bytes 3244032 | tf_op jit(solution)/shard_map/reduce_scatter | solution.py:22
  8.1 155.4 %copy-start.4 = (f32[2,176,512]{2,1,0:T(8,128)S(1)}, f32[2,176,512]{2,1,0:T(8,128)}, u32[]{:S(2)}) copy-start(f32[2,176,512]{2,1,0:T(8,128)} %param.23) | copy-start | bytes 2162692
  8.1 155.4 %copy-start.5 = (f32[2,176,512]{2,1,0:T(8,128)S(1)}, f32[2,176,512]{2,1,0:T(8,128)}, u32[]{:S(2)}) copy-start(f32[2,176,512]{2,1,0:T(8,128)} %param.20) | copy-start | bytes 2162692
  8.8 135.2 %reduce-scatter.8.cloned.1.call-start = ((), (), s32[]{:S(2)}) async-start(), calls=%async_computation.5 | async-start | bytes 3244032 | tf_op jit(solution)/shard_map/reduce_scatter | solution.py:22
  9.6 156.6 %copy-start.6 = (f32[2,64,1408]{2,1,0:T(8,128)S(1)}, f32[2,64,1408]{2,1,0:T(8,128)}, u32[]{:S(2)}) copy-start(f32[2,64,1408]{2,1,0:T(8,128)} %param.21) | copy-start | bytes 2162692
  9.6 156.6 %copy-start.7 = (f32[2,64,1408]{2,1,0:T(8,128)S(1)}, f32[2,64,1408]{2,1,0:T(8,128)}, u32[]{:S(2)}) copy-start(f32[2,64,1408]{2,1,0:T(8,128)} %param.18) | copy-start | bytes 2162692
  9.6 196.2 %all-gather.8.cloned.1.call-start = ((), (), s32[]{:S(2)}) async-start(), calls=%async_computation.8 | async-start | bytes 3244032 | tf_op jit(solution)/shard_map/all_gather | solution.py:28
  56.1 110.1 %copy-start.3 = (bf16[2,64,1408]{2,1,0:T(8,128)(2,1)S(1)}, bf16[2,64,1408]{2,1,0:T(8,128)(2,1)}, u32[]{:S(2)}) copy-start(bf16[2,64,1408]{2,1,0:T(8,128)(2,1)} %reduce-scatter.4.cloned.1.call-done) | copy-start | bytes 1081348
  166.0 2.8 copy-start.2
  166.0 2.8 copy-start.8
  166.1 80.3 %all-gather.4.cloned.1.call-start = ((), (), s32[]{:S(2)}) async-start(), calls=%async_computation.6 | async-start | bytes 3244032 | tf_op jit(solution)/shard_map/all_gather | solution.py:28
  168.7 118.2 %all-gather.6.cloned.1.call-start = ((), (), s32[]{:S(2)}) async-start(), calls=%async_computation.7 | async-start | bytes 3244032 | tf_op jit(solution)/shard_map/all_gather | solution.py:28
  286.9 3.8 %copy-start.1 = (bf16[2,512,1408]{2,1,0:T(8,128)(2,1)S(1)}, bf16[2,512,1408]{2,1,0:T(8,128)(2,1)}, u32[]{:S(2)}) copy-start(bf16[2,512,1408]{2,1,0:T(8,128)(2,1)} %all-gather.6.cloned.1.call-done) | copy-start | bytes 8650756
  290.7 2.9 copy-start
Sparse Core Ops, SparseCore 0:
  10.4 45.6 reduce-scatter.3
  58.5 41.5 reduce-scatter.5
  102.4 41.5 reduce-scatter.7
  166.2 39.5 all-gather.7
  207.8 38.4 all-gather.3
  248.4 38.4 all-gather.5
where the time goes:
time: 302 us
  waiting for transfers between devices  247 us (82%)
  between operations  16.9 us (6%)
  blocking collectives  16.4 us (5%)
  other arithmetic  13 us (4%)
  local copies, waits for them, and re-layouts  8.22 us (3%)
    reduce_scatter x3, waiting for transfers between devices, step(): lax.psum_scatter(t[0], 'dp', scatter_dimension=1, tiled=True)  129 us
    all_gather x3, waiting for transfers between devices, step(): whole = [lax.all_gather(one[0], 'dp', axis=1, tiled=True) for one in new]  115 us
    psum x1, blocking collectives, step(): squares = lax.psum(sum((jnp.sum(g * g) for g in gradients)), 'dp')  16.4 us
    unnamed x21, local copies, waits for them, and re-layouts  8.22 us
    convert_element_type x3, other arithmetic, adamw(): return ((w - 0.02 * step).astype(jnp.bfloat16), m, v)  7.65 us
  transfers between devices with their start and end apart: 6, of which 6 were waited for; matrix products, arithmetic and copies ran while one was open for 3% of the time, Pallas kernels for 0%

commit v1 on v0

v1 whole, which is shorter than its diff:
```python
import functools

import jax
import jax.numpy as jnp
from jax import lax
from jax.experimental import pallas as pl
from jax.experimental.pallas import tpu as pltpu
from jax.sharding import PartitionSpec as P

MESH = pl.DeviceIdType.MESH
TILE = 16


def adamw(w, m, v, g):
    m = 0.9 * m + 0.1 * g
    v = 0.95 * v + 0.05 * g * g
    step = m * lax.rsqrt(v + 1e-8) + 0.1 * w
    return (w - 0.02 * step).astype(jnp.bfloat16), m, v


def kernel(n, count, *refs):
    terms, weights, m_in, v_in = (refs[i : i + 3] for i in (0, 3, 6, 9))
    w_out, m_out, v_out = (refs[i : i + 3] for i in (12, 15, 18))
    held, came, own, m_own, v_own, total = (refs[i : i + 3] for i in (21, 24, 27, 30, 33, 36))
    parts, load_sem, own_sem, send_sem, recv_sem, part_send, part_recv = refs[39:]
    me = lax.axis_index("dp")
    right, left = lax.rem(me + 1, n), lax.rem(me + n - 1, n)
    rows = [m.shape[1] for m in m_in]
    half = n // 2
    towards = (right, left)
    hops = [[half - (layer != way) for layer in range(2)] for way in range(2)]

    def at(away):
        return lax.rem(me + away + n, n)

    def block(ref, k, layer, who):
        return ref.at[layer, pl.ds(pl.multiple_of(who * rows[k], rows[k]), rows[k])]

    def sign(way, away):
        return away if way == 0 else -away

    order = []
    for s in range(half + 1):
        for way in range(2):
            for layer in (way, 1 - way):
                j = sign(way, hops[way][layer] - s) % n
                if hops[way][layer] - s >= 0 and (layer, j) not in order:
                    order.append((layer, j))
    loads = {}
    for layer, j in order:
        for k in range(3):
            loads[layer, j, k] = pltpu.make_async_copy(
                block(terms[k].at[0], k, layer, at(j)), held[k].at[layer, j], load_sem.at[layer, j, k]
            )
            loads[layer, j, k].start()
    owns = []
    for k in range(3):
        owns += [
            pltpu.make_async_copy(weights[k].at[:, pl.ds(pl.multiple_of(me * rows[k], rows[k]), rows[k])], own[k], own_sem.at[0, k]),
            pltpu.make_async_copy(m_in[k], m_own[k], own_sem.at[1, k]),
            pltpu.make_async_copy(v_in[k], v_own[k], own_sem.at[2, k]),
        ]

    barrier = pltpu.get_barrier_semaphore()
    for peer in towards:
        pl.semaphore_signal(barrier, inc=1, device_id={"dp": peer}, device_id_type=MESH)
    pl.semaphore_wait(barrier, 2)

    def sum_copy(way, layer, s, k):
        slot = 2 * s + (layer != way)
        source = held[k].at[layer, sign(way, hops[way][layer]) % n] if s == 0 else came[k].at[way, 2 * (s - 1) + (layer != way)]
        return pltpu.make_async_remote_copy(
            src_ref=source,
            dst_ref=came[k].at[way, slot],
            send_sem=send_sem.at[way, slot, k],
            recv_sem=recv_sem.at[way, slot, k],
            device_id={"dp": towards[way]},
            device_id_type=MESH,
        )

    for which in range(2):
        for k in range(3):
            for way in range(2):
                layer = way if which == 0 else 1 - way
                loads[layer, sign(way, hops[way][layer]) % n, k].wait()
                sum_copy(way, layer, 0, k).start()
    for copy in owns:
        copy.start()

    squares = jnp.zeros((8, 128), jnp.float32)
    for s in range(half):
        for which in range(2):
            for k in range(3):
                for way in range(2):
                    layer = way if which == 0 else 1 - way
                    here = hops[way][layer] - 1 - s
                    if here < 0:
                        continue
                    slot = 2 * s + which
                    mine = came[k].at[way, slot]
                    sum_copy(way, layer, s, k).wait_recv()
                    if here > 0:
                        j = sign(way, here) % n
                        loads[layer, j, k].wait()
                        term = held[k].at[layer, j]

                        @pl.loop(0, rows[k] // TILE)
                        def _(t):
                            tile = pl.ds(pl.multiple_of(t * TILE, TILE), TILE)
                            mine[tile] = (mine[tile].astype(jnp.float32) + term[tile].astype(jnp.float32)).astype(jnp.bfloat16)

                        sum_copy(way, layer, s + 1, k).start()
                    elif which == 0:
                        other = came[k].at[1 - way, 2 * (s - 1) + 1]
                        loads[layer, 0, k].wait()
                        term, to = held[k].at[layer, 0], total[k].at[layer]

                        def add(t, squares):
                            tile = pl.ds(pl.multiple_of(t * TILE, TILE), TILE)
                            g = term[tile].astype(jnp.float32) + mine[tile].astype(jnp.float32) + other[tile].astype(jnp.float32)
                            g = g.astype(jnp.bfloat16)
                            to[tile] = g
                            g = g.astype(jnp.float32)
                            return squares + jnp.sum((g * g).reshape(-1, 8, to.shape[-1] // 128, 128), axis=(0, 2))

                        squares = lax.fori_loop(0, rows[k] // TILE, add, squares)

    parts[me] = squares
    for away in range(1, n):
        pltpu.make_async_remote_copy(
            src_ref=parts.at[me],
            dst_ref=parts.at[me],
            send_sem=part_send.at[away],
            recv_sem=part_recv.at[me],
            device_id={"dp": at(away)},
            device_id_type=MESH,
        ).start()
    for copy in owns:
        copy.wait()
    for way in range(2):
        for layer in range(2):
            for s in range(hops[way][layer]):
                for k in range(3):
                    sum_copy(way, layer, s, k).wait_send()
    for away in range(1, n):
        pltpu.make_async_remote_copy(
            src_ref=parts.at[at(away)],
            dst_ref=parts.at[at(away)],
            send_sem=part_send.at[away],
            recv_sem=part_recv.at[at(away)],
            device_id={"dp": at(away)},
            device_id_type=MESH,
        ).wait()
    everything = parts[0]
    for i in range(1, n):
        everything = everything + parts[i]
    factor = jnp.minimum(1.0, 0.5 * lax.rsqrt(jnp.sum(everything, keepdims=True) / count + 1e-30))

    def weight_copy(way, layer, s, k):
        ref = block(w_out[k], k, layer, at(-sign(way, s)))
        slot = 2 * s + (layer != way)
        return pltpu.make_async_remote_copy(
            src_ref=ref,
            dst_ref=ref,
            send_sem=send_sem.at[way, slot, k],
            recv_sem=recv_sem.at[way, slot, k],
            device_id={"dp": towards[way]},
            device_id_type=MESH,
        )

    for k in range(3):
        for layer in range(2):
            to = block(w_out[k], k, layer, me)

            @pl.loop(0, rows[k] // TILE)
            def _(t):
                tile = pl.ds(pl.multiple_of(t * TILE, TILE), TILE)
                g = total[k][layer, tile].astype(jnp.float32) * factor
                w, m, v = adamw(own[k][layer, tile].astype(jnp.float32), m_own[k][layer, tile], v_own[k][layer, tile], g)
                to[tile] = w
                m_out[k][layer, tile] = m
                v_out[k][layer, tile] = v

            for way in range(2):
                weight_copy(way, layer, 0, k).start()
    for s in range(half):
        for k in range(3):
            for layer in range(2):
                for way in range(2):
                    if s >= hops[way][layer]:
                        continue
                    slot = 2 * s + (layer != way)
                    ref = block(w_out[k], k, layer, at(-sign(way, s + 1)))
                    pltpu.make_async_remote_copy(
                        src_ref=ref,
                        dst_ref=ref,
                        send_sem=send_sem.at[way, slot, k],
                        recv_sem=recv_sem.at[way, slot, k],
                        device_id={"dp": towards[way]},
                        device_id_type=MESH,
                    ).wait_recv()
                    if s + 1 < hops[way][layer]:
                        weight_copy(way, layer, s + 1, k).start()
    for way in range(2):
        for layer in range(2):
            for s in range(hops[way][layer]):
                for k in range(3):
                    weight_copy(way, layer, s, k).wait_send()


def flush(*refs):
    sem = refs[-1]
    half = len(refs) // 2
    copies = [pltpu.make_async_copy(refs[i], refs[half + i], sem.at[i]) for i in range(half)]
    for copy in copies:
        copy.start()
    for copy in copies:
        copy.wait()


def solution(mesh):
    def step(*arrays):
        n = lax.axis_size("dp")
        terms, weights, m, v = (arrays[i : i + 3] for i in (0, 3, 6, 9))
        count = sum(w.size for w in weights)
        shapes = [(w.shape, w.dtype) for w in weights] + [(x.shape, x.dtype) for x in (*m, *v)]
        blocks = [(one.shape[1], one.shape[2]) for one in m]
        half = n // 2
        outs = pl.pallas_call(
            functools.partial(kernel, n, count),
            name="step",
            out_shape=[pltpu.VMEM(s, d) for s, d in shapes],
            in_specs=[pl.BlockSpec(memory_space=pl.ANY)] * 12,
            out_specs=[pl.BlockSpec(memory_space=pltpu.VMEM)] * 9,
            scratch_shapes=[
                *(pltpu.VMEM((2, n, *b), jnp.bfloat16) for b in blocks),
                *(pltpu.VMEM((2, 2 * half - 1, *b), jnp.bfloat16) for b in blocks),
                *(pltpu.VMEM((2, *b), jnp.bfloat16) for b in blocks),
                *(pltpu.VMEM((2, *b), jnp.float32) for b in blocks),
                *(pltpu.VMEM((2, *b), jnp.float32) for b in blocks),
                *(pltpu.VMEM((2, *b), jnp.bfloat16) for b in blocks),
                pltpu.VMEM((n, 8, 128), jnp.float32),
                pltpu.SemaphoreType.DMA((2, n, 3)),
                pltpu.SemaphoreType.DMA((3, 3)),
                pltpu.SemaphoreType.DMA((2, 2 * half - 1, 3)),
                pltpu.SemaphoreType.DMA((2, 2 * half - 1, 3)),
                pltpu.SemaphoreType.DMA((n,)),
                pltpu.SemaphoreType.DMA((n,)),
            ],
            compiler_params=pltpu.CompilerParams(collective_id=0, has_side_effects=True, vmem_limit_bytes=44 * 2**20),
        )(*arrays)
        return tuple(outs)

    all_of, cut = P(None, None, None), P(None, "dp", None)
    return jax.shard_map(
        step,
        mesh=mesh,
        in_specs=(P(("rep", "dp"), None, None, None),) * 3 + (all_of,) * 3 + (cut,) * 6,
        out_specs=(P("rep", None, None),) * 3 + (P("rep", "dp", None),) * 6,
        check_vma=False,
    )
```

time: 302 us -> 189 us (0.63)
  waiting for transfers between devices: 247 us -> 0 us
  Pallas kernels: 0 us -> 179 us
  blocking collectives: 16.4 us -> 0 us
  between operations: 16.9 us -> 0.66 us
  other arithmetic: 13 us -> 0 us
    pallas_call x0 -> x1, Pallas kernels: none -> 179 us  [step(): pl.pallas_call(functools.partial(kernel, n, count), name='step', out_shap...]
    reduce_scatter x3 -> x0, waiting for transfers between devices: 129 us -> none  [step(): lax.psum_scatter(t[0], 'dp', scatter_dimension=1, tiled=True)]
    all_gather x3 -> x0, waiting for transfers between devices: 115 us -> none  [step(): whole = [lax.all_gather(one[0], 'dp', axis=1, tiled=True) for one in new]]
    psum x1 -> x0, blocking collectives: 16.4 us -> none  [step(): squares = lax.psum(sum((jnp.sum(g * g) for g in gradients)), 'dp')]
    convert_element_type x3 -> x0, other arithmetic: 7.65 us -> none  [adamw(): return ((w - 0.02 * step).astype(jnp.bfloat16), m, v)]
    reduce_sum x3 -> x0, other arithmetic: 5.39 us -> none  [step(): squares = lax.psum(sum((jnp.sum(g * g) for g in gradients)), 'dp')]
    unnamed x21 -> x9, local copies, waits for them, and re-layouts: 8.22 us -> 9.88 us
  transfers between devices with their start and end apart: 6 -> 0, of which waited for: 6 -> 0; matrix products, arithmetic and copies ran while one was open for 3% -> 0% of each run, Pallas kernels for 0% -> 0%
where the time goes in v1:
time: 189 us
  Pallas kernels  179 us (95%)
  local copies, waits for them, and re-layouts  9.88 us (5%)
    pallas_call x1, Pallas kernels, step(): pl.pallas_call(functools.partial(kernel, n, count), name='step', out_shap...  179 us
    unnamed x9, local copies, waits for them, and re-layouts  9.88 us

profile of v1, /device:TPU:22, one launch (start us, length us, event | category | flops | bytes accessed | tf_op | source)
XLA Modules:
  0.0 189.3 jit_solution(18075779808472560000)
XLA Ops:
  0.6 178.8 %step.1 = (bf16[2,512,1408]{2,1,0:T(8,128)(2,1)S(1)}, bf16[2,512,1408]{2,1,0:T(8,128)(2,1)S(1)}, bf16[2,1408,512]{2,1,0:T(8,128)(2,1)S(1)}, f32[2,64,1408]{2,1,0...) custom-call(bf16[1,2,512,1408]{3,2,1,0:T(8,128)(2,1)} %refs_0_.1, ...), custom_call_target="tpu_custom_call" | custom-call | tf_op jit(solution)/shard_map/step/pallas_call | solution.py:229
  179.5 1.6 copy.30
  181.0 0.9 copy.33
  181.9 0.9 copy.34
  182.7 0.9 copy.35
  183.6 0.9 copy.36
  184.5 0.9 copy.37
  185.3 0.9 copy.38
  186.2 1.6 copy.31
  187.8 1.6 copy.32

commit v2 on v1

v2 whole, which is shorter than its diff:
```python
import functools

import jax
import jax.numpy as jnp
from jax import lax
from jax.experimental import pallas as pl
from jax.experimental.pallas import tpu as pltpu
from jax.sharding import PartitionSpec as P

MESH = pl.DeviceIdType.MESH
TILE = 16


def adamw(w, m, v, g):
    m = 0.9 * m + 0.1 * g
    v = 0.95 * v + 0.05 * g * g
    step = m * lax.rsqrt(v + 1e-8) + 0.1 * w
    return (w - 0.02 * step).astype(jnp.bfloat16), m, v


def pieces(rows):
    head, tail = TILE, 2 * TILE
    return [(0, 0, head), (0, head, rows[0] - head), (1, 0, rows[1]), (2, 0, rows[2] - tail), (2, rows[2] - tail, tail)]


def kernel(n, count, *refs):
    terms, weights, m_in, v_in = (refs[i : i + 3] for i in (0, 3, 6, 9))
    w_out, m_out, v_out = (refs[i : i + 3] for i in (12, 15, 18))
    held, came, own, m_own, v_own, total = (refs[i : i + 3] for i in (21, 24, 27, 30, 33, 36))
    parts, load_sem, own_sem, send_sem, recv_sem, part_send, part_recv = refs[39:]
    me = lax.axis_index("dp")
    rows = [m.shape[1] for m in m_in]
    cuts = pieces(rows)
    half = n // 2

    def at(away):
        return lax.rem(me + away + n, n)

    towards = (at(1), at(-1))
    hops = [[half - (layer != way) for layer in range(2)] for way in range(2)]

    barrier = pltpu.get_barrier_semaphore()
    for peer in towards:
        pl.semaphore_signal(barrier, inc=1, device_id={"dp": peer}, device_id_type=MESH)

    def block(ref, layer, who, k, first=0, size=None):
        return ref.at[layer, pl.ds(pl.multiple_of(who * rows[k] + first, TILE), size or rows[k])]

    def sign(way, away):
        return away if way == 0 else -away

    order = [(way, sign(way, half) % n) for way in range(2)] + [(1 - way, sign(way, half - 1) % n) for way in range(2)]
    order = list(dict.fromkeys(order))
    for j in [j for d in range(half - 1, -1, -1) for j in (d, n - d)]:
        for layer in range(2):
            if (layer, j % n) not in order:
                order.append((layer, j % n))
    loads = {
        (layer, j, k): pltpu.make_async_copy(block(terms[k].at[0], layer, at(j), k), held[k].at[layer, j], load_sem.at[layer, j, k])
        for layer, j in order
        for k in range(3)
    }
    owns = []
    for k in range(3):
        owns += [
            pltpu.make_async_copy(weights[k].at[:, pl.ds(pl.multiple_of(me * rows[k], rows[k]), rows[k])], own[k], own_sem.at[0, k]),
            pltpu.make_async_copy(m_in[k], m_own[k], own_sem.at[1, k]),
            pltpu.make_async_copy(v_in[k], v_own[k], own_sem.at[2, k]),
        ]
    first = [(layer, j, k) for layer, j in order[:4] for k in range(3)]
    for key in first:
        loads[key].start()
    with jax.named_scope("barrier"):
        pl.semaphore_wait(barrier, 2)

    def sum_copy(way, layer, s, p):
        k, start, size = cuts[p]
        slot = 2 * s + (layer != way)
        source = held[k].at[layer, sign(way, hops[way][layer]) % n] if s == 0 else came[k].at[way, 2 * (s - 1) + (layer != way)]
        return pltpu.make_async_remote_copy(
            src_ref=source.at[pl.ds(start, size)],
            dst_ref=came[k].at[way, slot, pl.ds(start, size)],
            send_sem=send_sem.at[way, slot, p],
            recv_sem=recv_sem.at[way, slot, p],
            device_id={"dp": towards[way]},
            device_id_type=MESH,
        )

    waited = set()
    def loaded(*key):
        if key not in waited:
            waited.add(key)
            loads[key].wait()

    with jax.named_scope("first"):
        for which in range(2):
            for p, (k, _, _) in enumerate(cuts):
                for way in range(2):
                    layer = way if which == 0 else 1 - way
                    loaded(layer, sign(way, hops[way][layer]) % n, k)
                    sum_copy(way, layer, 0, p).start()
        for key, copy in loads.items():
            if key not in first:
                copy.start()
        for copy in owns:
            copy.start()

    squares = jnp.zeros((8, 128), jnp.float32)
    for s in range(half):
        for which in range(2):
            for p, (k, start, size) in enumerate(cuts):
                for way in range(2):
                    layer = way if which == 0 else 1 - way
                    here = hops[way][layer] - 1 - s
                    if here < 0:
                        continue
                    slot = 2 * s + which
                    mine = came[k].at[way, slot]
                    with jax.named_scope(f"recv{s}{which}{p}{way}"):
                        sum_copy(way, layer, s, p).wait_recv()
                    if here > 0:
                        j = sign(way, here) % n
                        loaded(layer, j, k)
                        term = held[k].at[layer, j]

                        @pl.loop(0, size // TILE)
                        def _(t):
                            tile = pl.ds(pl.multiple_of(start + t * TILE, TILE), TILE)
                            mine[tile] = (mine[tile].astype(jnp.float32) + term[tile].astype(jnp.float32)).astype(jnp.bfloat16)

                        sum_copy(way, layer, s + 1, p).start()
                    elif which == 0:
                        other = came[k].at[1 - way, 2 * (s - 1) + 1]
                        loaded(layer, 0, k)
                        term, to = held[k].at[layer, 0], total[k].at[layer]

                        def add(t, squares):
                            tile = pl.ds(pl.multiple_of(start + t * TILE, TILE), TILE)
                            g = term[tile].astype(jnp.float32) + mine[tile].astype(jnp.float32) + other[tile].astype(jnp.float32)
                            g = g.astype(jnp.bfloat16)
                            to[tile] = g
                            g = g.astype(jnp.float32)
                            g = g * g
                            for i in range(TILE // 8):
                                for c in range(g.shape[1] // 128):
                                    squares = squares + g[8 * i : 8 * i + 8, 128 * c : 128 * c + 128]
                            return squares

                        squares = lax.fori_loop(0, size // TILE, add, squares)

    def part_copy(away, sender):
        ref = parts.at[pl.ds(sender, 1)]
        return pltpu.make_async_remote_copy(
            src_ref=ref,
            dst_ref=ref,
            send_sem=part_send.at[away % n],
            recv_sem=part_recv.at[sender],
            device_id={"dp": at(away)},
            device_id_type=MESH,
        )

    far = sorted(range(1, n), key=lambda away: -min(away, n - away))
    with jax.named_scope("exchange"):
        parts[pl.ds(me, 1)] = jnp.sum(squares, axis=0, keepdims=True)
        for away in far:
            part_copy(away, me).start()
        for copy in owns:
            copy.wait()
        for way in range(2):
            for layer in range(2):
                for s in range(hops[way][layer]):
                    for p in range(len(cuts)):
                        sum_copy(way, layer, s, p).wait_send()
        for away in far[::-1]:
            part_copy(away, at(away)).wait()
    factor = jnp.minimum(1.0, 0.5 * lax.rsqrt(jnp.sum(parts[...], keepdims=True) / count + 1e-30))

    def weight_copy(way, layer, s, p, sender):
        k, start, size = cuts[p]
        ref = block(w_out[k], layer, sender, k, start, size)
        slot = 2 * s + (layer != way)
        return pltpu.make_async_remote_copy(
            src_ref=ref,
            dst_ref=ref,
            send_sem=send_sem.at[way, slot, p],
            recv_sem=recv_sem.at[way, slot, p],
            device_id={"dp": towards[way]},
            device_id_type=MESH,
        )

    for p, (k, start, size) in enumerate(cuts):
        for layer in range(2):
            to = block(w_out[k], layer, me, k)

            with jax.named_scope(f"adamw{p}{layer}"):

                @pl.loop(0, size // TILE)
                def _(t):
                    tile = pl.ds(pl.multiple_of(start + t * TILE, TILE), TILE)
                    g = total[k][layer, tile].astype(jnp.float32) * factor
                    w, m, v = adamw(own[k][layer, tile].astype(jnp.float32), m_own[k][layer, tile], v_own[k][layer, tile], g)
                    to[tile] = w
                    m_out[k][layer, tile] = m
                    v_out[k][layer, tile] = v

            for way in range(2):
                weight_copy(way, layer, 0, p, me).start()
    for s in range(half):
        for p in range(len(cuts)):
            for layer in range(2):
                for way in range(2):
                    if s >= hops[way][layer]:
                        continue
                    with jax.named_scope(f"get{s}{p}{layer}{way}"):
                        weight_copy(way, layer, s, p, at(-sign(way, s + 1))).wait_recv()
                    if s + 1 < hops[way][layer]:
                        weight_copy(way, layer, s + 1, p, at(-sign(way, s + 1))).start()
    with jax.named_scope("ends"):
        for way in range(2):
            for layer in range(2):
                for s in range(hops[way][layer]):
                    for p in range(len(cuts)):
                        weight_copy(way, layer, s, p, at(-sign(way, s))).wait_send()


def flush(*refs):
    sem = refs[-1]
    half = len(refs) // 2
    copies = [pltpu.make_async_copy(refs[i], refs[half + i], sem.at[i]) for i in range(half)]
    for copy in copies:
        copy.start()
    for copy in copies:
        copy.wait()


def solution(mesh):
    def step(*arrays):
        n = lax.axis_size("dp")
        terms, weights, m, v = (arrays[i : i + 3] for i in (0, 3, 6, 9))
        count = sum(w.size for w in weights)
        shapes = [(w.shape, w.dtype) for w in weights] + [(x.shape, x.dtype) for x in (*m, *v)]
        blocks = [(one.shape[1], one.shape[2]) for one in m]
        half, cuts = n // 2, len(pieces([b[0] for b in blocks]))
        outs = pl.pallas_call(
            functools.partial(kernel, n, count),
            name="step",
            out_shape=[pltpu.VMEM(s, d) for s, d in shapes],
            in_specs=[pl.BlockSpec(memory_space=pl.ANY)] * 12,
            out_specs=[pl.BlockSpec(memory_space=pltpu.VMEM)] * 9,
            scratch_shapes=[
                *(pltpu.VMEM((2, n, *b), jnp.bfloat16) for b in blocks),
                *(pltpu.VMEM((2, 2 * half - 1, *b), jnp.bfloat16) for b in blocks),
                *(pltpu.VMEM((2, *b), jnp.bfloat16) for b in blocks),
                *(pltpu.VMEM((2, *b), jnp.float32) for b in blocks),
                *(pltpu.VMEM((2, *b), jnp.float32) for b in blocks),
                *(pltpu.VMEM((2, *b), jnp.bfloat16) for b in blocks),
                pltpu.VMEM((n, 128), jnp.float32),
                pltpu.SemaphoreType.DMA((2, n, 3)),
                pltpu.SemaphoreType.DMA((3, 3)),
                pltpu.SemaphoreType.DMA((2, 2 * half - 1, cuts)),
                pltpu.SemaphoreType.DMA((2, 2 * half - 1, cuts)),
                pltpu.SemaphoreType.DMA((n,)),
                pltpu.SemaphoreType.DMA((n,)),
            ],
            compiler_params=pltpu.CompilerParams(collective_id=0, has_side_effects=True, vmem_limit_bytes=44 * 2**20),
        )(*arrays)
        return tuple(
            pl.pallas_call(
                flush,
                name="flush",
                out_shape=[jax.ShapeDtypeStruct(s, d) for s, d in shapes],
                in_specs=[pl.BlockSpec(memory_space=pltpu.VMEM)] * 9,
                out_specs=[pl.BlockSpec(memory_space=pl.ANY)] * 9,
                scratch_shapes=[pltpu.SemaphoreType.DMA((9,))],
                compiler_params=pltpu.CompilerParams(vmem_limit_bytes=2**20),
            )(*outs)
        )

    all_of, cut = P(None, None, None), P(None, "dp", None)
    return jax.shard_map(
        step,
        mesh=mesh,
        in_specs=(P(("rep", "dp"), None, None, None),) * 3 + (all_of,) * 3 + (cut,) * 6,
        out_specs=(P("rep", None, None),) * 3 + (P("rep", "dp", None),) * 6,
        check_vma=False,
    )
```

time: 189 us -> 184 us (0.974)
  local copies, waits for them, and re-layouts: 9.88 us -> 0 us
  Pallas kernels: 179 us -> 183 us
    unnamed x9 -> x0, local copies, waits for them, and re-layouts: 9.88 us -> none
    pallas_call x0 -> x1, Pallas kernels: none -> 4.79 us  [step(): pl.pallas_call(flush, name='flush', out_shape=[jax.ShapeDtypeStruct(s, d)...]
where the time goes in v2:
time: 184 us
  Pallas kernels  183 us (99%)
    pallas_call x1, Pallas kernels, step(): pl.pallas_call(functools.partial(kernel, n, count), name='step', out_shap...  179 us
    pallas_call x1, Pallas kernels, step(): pl.pallas_call(flush, name='flush', out_shape=[jax.ShapeDtypeStruct(s, d)...  4.79 us

profile of v2, /device:TPU:22, one launch (start us, length us, event | category | flops | bytes accessed | tf_op | source)
XLA Modules:
  0.0 184.0 jit_solution(3961956963170127928)
XLA Ops:
  0.6 178.6 %step.1 = (bf16[2,512,1408]{2,1,0:T(8,128)(2,1)S(1)}, bf16[2,512,1408]{2,1,0:T(8,128)(2,1)S(1)}, bf16[2,1408,512]{2,1,0:T(8,128)(2,1)S(1)}, f32[2,64,1408]{2,1,0...) custom-call(bf16[1,2,512,1408]{3,2,1,0:T(8,128)(2,1)} %refs_0_.1, ...), custom_call_target="tpu_custom_call" | custom-call | tf_op jit(solution)/shard_map/step/pallas_call | solution.py:244
  179.2 4.8 %flush.1 = (bf16[2,512,1408]{2,1,0:T(8,128)(2,1)}, bf16[2,512,1408]{2,1,0:T(8,128)(2,1)}, bf16[2,1408,512]{2,1,0:T(8,128)(2,1)}, f32[2,64,1408]{2,1,0:T(8,128)},...) custom-call(bf16[2,512,1408]{2,1,0:T(8,128)(2,1)S(1)} %get-tuple-ele, ...), custom_call_target="tpu_custom_call" | custom-call | tf_op jit(solution)/shard_map/flush/pallas_call | solution.py:268

commit v3 on v0

v3 whole, which is shorter than its diff:
```python
import functools

import jax
import jax.numpy as jnp
from jax import lax
from jax.experimental import pallas as pl
from jax.experimental.pallas import tpu as pltpu
from jax.sharding import PartitionSpec as P

MESH = pl.DeviceIdType.MESH
TILE = 16
LATER = 13500


def adamw(w, m, v, g):
    m = 0.9 * m + 0.1 * g
    v = 0.95 * v + 0.05 * g * g
    step = m * lax.rsqrt(v + 1e-8) + 0.1 * w
    return (w - 0.02 * step).astype(jnp.bfloat16), m, v


class Gather:
    def __init__(self, n, towards, layers, hops, send_sem, recv_sem):
        self.n, self.towards, self.layers, self.hops = n, towards, layers, hops
        self.send_sem, self.recv_sem = send_sem, recv_sem
        self.me = lax.axis_index("dp")

    def behind(self, way, s):
        return lax.rem(self.me + (-s if way == 0 else s) + self.n, self.n)

    def copy(self, ref, way, short, s, p, sender, rows, start=0, size=None, source=None):
        to = ref.at[self.layers[way][short], pl.ds(pl.multiple_of(sender * rows + start, TILE), size or rows)]
        return pltpu.make_async_remote_copy(
            src_ref=to if source is None else source,
            dst_ref=to,
            send_sem=self.send_sem.at[way, short, p],
            recv_sem=self.recv_sem.at[way, 2 * s + short, p],
            device_id={"dp": self.towards[way]},
            device_id_type=MESH,
        )

    def forward(self, pieces, own=None):
        for s in range(self.hops[0]):
            for p, (ref, *piece) in enumerate(pieces):
                rows, start, size = piece
                for short in range(2):
                    for way in range(2):
                        if s >= self.hops[short]:
                            continue

                        def copy(step, behind, source=None):
                            return self.copy(ref, way, short, step, p, self.behind(way, behind), rows, start, size, source)

                        with jax.named_scope(f"get{s}{p}{short}{way}"):
                            copy(s, s + 1).wait_recv()
                        mine = own.at[self.layers[way][short], pl.ds(start, size)] if own is not None and s == 0 else None
                        copy(s, s, mine).wait_send()
                        if s + 1 < self.hops[short]:
                            copy(s + 1, s + 1).start()


def kernel(n, count, *refs):
    terms, weights, m_in, v_in = (refs[i : i + 3] for i in (0, 3, 6, 9))
    w_out, m_out, v_out = (refs[i : i + 3] for i in (12, 15, 18))
    raw, held, came, own, m_own, v_own, total = (refs[i : i + 3] for i in range(21, 42, 3))
    parts, load_sem, own_sem, send_sem, recv_sem, part_sem = refs[42:]
    me = lax.axis_index("dp")
    rows = [m.shape[1] for m in m_in]
    half = n // 2

    def at(away):
        return lax.rem(me + away + n, n)

    def sign(way, away):
        return away if way == 0 else -away

    def block(ref, layer, who, k):
        return ref.at[layer, pl.ds(pl.multiple_of(who * rows[k], rows[k]), rows[k])]

    towards = (at(1), at(-1))
    layers = [[way, 1 - way] for way in range(2)]
    hops = [half, half - 1]

    barrier = pltpu.get_barrier_semaphore()
    for peer in towards:
        pl.semaphore_signal(barrier, inc=1, device_id={"dp": peer}, device_id_type=MESH)

    def first(way, short, k, sem):
        source = block(terms[k].at[0], layers[way][short], at(sign(way, hops[short])), k)
        return pltpu.make_async_copy(source, raw[k].at[way, short], load_sem.at[sem])

    rest = [pltpu.make_async_copy(terms[k].at[0], held[k], load_sem.at[k]) for k in range(3)]
    owns = [
        pltpu.make_async_copy(source, to, own_sem.at[i, k])
        for k in range(3)
        for i, (source, to) in enumerate(
            [(weights[k].at[:, pl.ds(pl.multiple_of(me * rows[k], rows[k]), rows[k])], own[k]), (m_in[k], m_own[k]), (v_in[k], v_own[k])]
        )
    ]
    for way in range(2):
        first(way, 0, 0, 3).start()
    pl.semaphore_wait(barrier, 2)
    for k in range(3):
        for short in range(k == 0, 2):
            for way in range(2):
                first(way, short, k, k).start()

    @pl.when(lax.rem(lax.axis_index("rep"), 2) == 1)
    def _():
        pl.delay(LATER)

    def send(way, short, s, k, source, to):
        return pltpu.make_async_remote_copy(
            src_ref=source,
            dst_ref=to,
            send_sem=send_sem.at[way, short, k],
            recv_sem=recv_sem.at[way, 2 * s + short, k],
            device_id={"dp": towards[way]},
            device_id_type=MESH,
        )

    def sum_copy(way, short, s, k):
        source = raw[k].at[way, short] if s == 0 else came[k].at[way, 2 * (s - 1) + short]
        return send(way, short, s, k, source, came[k].at[way, 2 * s + short])

    with jax.named_scope("first"):
        for k in range(3):
            for short in range(2):
                if k == 0 or not short:
                    ready = raw[k] if k else raw[k].at[:, short]
                    pltpu.make_async_copy(ready, ready, load_sem.at[0 if short else (3, 1, 2)[k]]).wait()
                for way in range(2):
                    sum_copy(way, short, 0, k).start()
            rest[k].start()
        for copy in owns:
            copy.start()

    squares = jnp.zeros((8, 128), jnp.float32)
    waited = set()
    for s in range(half):
        for k in range(3):
            for short in range(2):
                for way in range(2):
                    here = hops[short] - 1 - s
                    if here < 0:
                        continue
                    layer = layers[way][short]
                    mine = came[k].at[way, 2 * s + short]
                    with jax.named_scope(f"recv{s}{k}{short}{way}"):
                        sum_copy(way, short, s, k).wait_recv()
                    if k not in waited:
                        waited.add(k)
                        rest[k].wait()
                    term = block(held[k], layer, at(sign(way, here)), k)
                    if here > 0:

                        @pl.loop(0, rows[k] // TILE)
                        def _(t):
                            tile = pl.ds(pl.multiple_of(t * TILE, TILE), TILE)
                            mine[tile] = (mine[tile].astype(jnp.float32) + term[tile].astype(jnp.float32)).astype(jnp.bfloat16)

                        sum_copy(way, short, s, k).wait_send()
                        sum_copy(way, short, s + 1, k).start()
                    elif not short:
                        other, to = came[k].at[1 - way, 2 * (s - 1) + 1], total[k].at[layer]

                        def add(t, squares):
                            tile = pl.ds(pl.multiple_of(t * TILE, TILE), TILE)
                            g = term[tile].astype(jnp.float32) + mine[tile].astype(jnp.float32) + other[tile].astype(jnp.float32)
                            g = g.astype(jnp.bfloat16)
                            to[tile] = g
                            g = g.astype(jnp.float32)
                            g = g * g
                            for i in range(TILE // 8):
                                for c in range(g.shape[1] // 128):
                                    squares = squares + g[8 * i : 8 * i + 8, 128 * c : 128 * c + 128]
                            return squares

                        squares = lax.fori_loop(0, rows[k] // TILE, add, squares)

    def part_copy(away, sender):
        ref = parts.at[pl.ds(sender, 1)]
        return pltpu.make_async_remote_copy(
            src_ref=ref,
            dst_ref=ref,
            send_sem=part_sem.at[0],
            recv_sem=part_sem.at[1],
            device_id={"dp": at(away)},
            device_id_type=MESH,
        )

    with jax.named_scope("exchange"):
        parts[pl.ds(me, 1)] = jnp.sum(squares, axis=0, keepdims=True)
        for away in sorted(range(1, n), key=lambda away: -min(away, n - away)):
            part_copy(away, me).start()
        for copy in owns:
            copy.wait()
        for way in range(2):
            for short in range(2):
                for k in range(3):
                    sum_copy(way, short, hops[short] - 1, k).wait_send()
        others = parts.at[pl.ds(0, n - 1)]
        for i in range(2):
            pltpu.make_async_copy(others, others, part_sem.at[i]).wait()
    factor = jnp.minimum(1.0, 0.5 * lax.rsqrt(jnp.sum(parts[...], keepdims=True) / count + 1e-30))

    gather = Gather(n, towards, layers, hops, send_sem, recv_sem)
    last = len(weights) - 1
    for k in range(3):
        for layer in range(2):
            to = w_out[k].at[layer] if k == last else block(w_out[k], layer, me, k)

            with jax.named_scope(f"adamw{k}{layer}"):

                @pl.loop(0, rows[k] // TILE)
                def _(t):
                    tile = pl.ds(pl.multiple_of(t * TILE, TILE), TILE)
                    g = total[k][layer, tile].astype(jnp.float32) * factor
                    w, m, v = adamw(own[k][layer, tile].astype(jnp.float32), m_own[k][layer, tile], v_own[k][layer, tile], g)
                    to[tile] = w
                    m_out[k][layer, tile] = m
                    v_out[k][layer, tile] = v

            if k < last:
                for way in range(2):
                    gather.copy(w_out[k], way, int(layer != way), 0, k, me, rows[k]).start()
    gather.forward([(w_out[k], rows[k], 0, rows[k]) for k in range(last)])


def kernel_of_the_last(n, own, token, out, send_sem, recv_sem):
    del token
    me = lax.axis_index("dp")
    towards = (lax.rem(me + 1, n), lax.rem(me + n - 1, n))
    rows = own.shape[1]
    cut = rows // 2 // TILE * TILE
    cuts = [(0, rows - cut), (rows - cut, cut)]
    barrier = pltpu.get_barrier_semaphore()
    for peer in towards:
        pl.semaphore_signal(barrier, inc=1, device_id={"dp": peer}, device_id_type=MESH)
    first = pl.multiple_of(me * rows, rows)

    @pl.loop(0, rows // TILE)
    def _(t):
        tile = pl.multiple_of(t * TILE, TILE)
        for layer in range(2):
            out[layer, pl.ds(pl.multiple_of(first + tile, TILE), TILE)] = own[layer, pl.ds(tile, TILE)]

    pl.semaphore_wait(barrier, 2)
    gather = Gather(n, towards, [[way, 1 - way] for way in range(2)], [n // 2, n // 2 - 1], send_sem, recv_sem)
    for p, (start, size) in enumerate(cuts):
        for short in range(2):
            for way in range(2):
                source = own.at[gather.layers[way][short], pl.ds(start, size)]
                gather.copy(out, way, short, 0, p, me, rows, start, size, source).start()
    gather.forward([(out, rows, *cut) for cut in cuts], own)


def flush(count, *refs):
    sem, tokens = refs[-1], refs[2 * count : -1]
    copies = [pltpu.make_async_copy(refs[i], refs[count + i], sem.at[i]) for i in range(count)]
    for copy in copies:
        copy.start()
    for token in tokens:
        token[...] = jnp.zeros_like(token)
    for copy in copies:
        copy.wait()


def flushed(arrays, *tokens):
    count = len(arrays)
    return pl.pallas_call(
        functools.partial(flush, count),
        name="flush",
        out_shape=[*(jax.ShapeDtypeStruct(a.shape, a.dtype) for a in arrays), *tokens],
        in_specs=[pl.BlockSpec(memory_space=pltpu.VMEM)] * count,
        out_specs=[pl.BlockSpec(memory_space=pl.ANY)] * count + [pl.BlockSpec(memory_space=pltpu.VMEM)] * len(tokens),
        scratch_shapes=[pltpu.SemaphoreType.DMA((count,))],
        compiler_params=pltpu.CompilerParams(vmem_limit_bytes=2**20),
    )(*arrays)


def solution(mesh):
    def step(*arrays):
        n = lax.axis_size("dp")
        terms, weights, m, v = (arrays[i : i + 3] for i in (0, 3, 6, 9))
        count = sum(w.size for w in weights)
        shapes = [(w.shape, w.dtype) for w in weights[:-1]] + [(m[-1].shape, weights[-1].dtype)] + [(x.shape, x.dtype) for x in (*m, *v)]
        blocks = [(one.shape[1], one.shape[2]) for one in m]
        half = n // 2
        outs = pl.pallas_call(
            functools.partial(kernel, n, count),
            name="step",
            out_shape=[pltpu.VMEM(s, d) for s, d in shapes],
            in_specs=[pl.BlockSpec(memory_space=pl.ANY)] * 12,
            out_specs=[pl.BlockSpec(memory_space=pltpu.VMEM)] * 9,
            scratch_shapes=[
                *(pltpu.VMEM((2, 2, *b), jnp.bfloat16) for b in blocks),
                *(pltpu.VMEM(w.shape, jnp.bfloat16) for w in weights),
                *(pltpu.VMEM((2, 2 * half - 1, *b), jnp.bfloat16) for b in blocks),
                *(pltpu.VMEM((2, *b), jnp.bfloat16) for b in blocks),
                *(pltpu.VMEM((2, *b), jnp.float32) for b in blocks * 2),
                *(pltpu.VMEM((2, *b), jnp.bfloat16) for b in blocks),
                pltpu.VMEM((n, 128), jnp.float32),
                pltpu.SemaphoreType.DMA((4,)),
                pltpu.SemaphoreType.DMA((3, 3)),
                pltpu.SemaphoreType.DMA((2, 2, 3)),
                pltpu.SemaphoreType.DMA((2, 2 * half - 1, 3)),
                pltpu.SemaphoreType.DMA((2,)),
            ],
            compiler_params=pltpu.CompilerParams(collective_id=0, has_side_effects=True, vmem_limit_bytes=48 * 2**20),
        )(*arrays)
        *whole, own, m0, m1, m2, v0, v1, v2 = outs
        *done, token = flushed([*whole, m0, m1, m2, v0, v1, v2], pltpu.VMEM((8, 128), jnp.float32))
        last = pl.pallas_call(
            functools.partial(kernel_of_the_last, n),
            name="last",
            out_shape=pltpu.VMEM(weights[-1].shape, weights[-1].dtype),
            in_specs=[pl.BlockSpec(memory_space=pltpu.VMEM)] * 2,
            out_specs=pl.BlockSpec(memory_space=pltpu.VMEM),
            scratch_shapes=[pltpu.SemaphoreType.DMA((2, 2, 2)), pltpu.SemaphoreType.DMA((2, 2 * half - 1, 2))],
            compiler_params=pltpu.CompilerParams(collective_id=1, has_side_effects=True, vmem_limit_bytes=2**20),
        )(own, token)
        return (*done[: len(whole)], *flushed([last]), *done[len(whole) :])

    all_of, cut = P(None, None, None), P(None, "dp", None)
    return jax.shard_map(
        step,
        mesh=mesh,
        in_specs=(P(("rep", "dp"), None, None, None),) * 3 + (all_of,) * 3 + (cut,) * 6,
        out_specs=(P("rep", None, None),) * 3 + (P("rep", "dp", None),) * 6,
        check_vma=False,
    )
```

time: 302 us -> 176 us (0.58)
  the two profiles are of different devices: /device:TPU:22 before, /device:TPU:21 now
where the time goes in v3:
time: 176 us
  Pallas kernels  175 us (99%)
    pallas_call x1, Pallas kernels, step(): pl.pallas_call(functools.partial(kernel, n, count), name='step', out_shap...  148 us
    pallas_call x1, Pallas kernels, step(): pl.pallas_call(functools.partial(kernel_of_the_last, n), name='last', out...  21.3 us
    pallas_call x2, Pallas kernels, flushed(): pl.pallas_call(functools.partial(flush, count), name='flush', out_shape=[...  5.5 us

profile of v3, /device:TPU:21, one launch (start us, length us, event | category | flops | bytes accessed | tf_op | source)
XLA Modules:
  0.0 175.8 jit_solution(12079561411889949638)
XLA Ops:
  0.6 148.3 %step.1 = (bf16[2,512,1408]{2,1,0:T(8,128)(2,1)S(1)}, bf16[2,512,1408]{2,1,0:T(8,128)(2,1)S(1)}, bf16[2,176,512]{2,1,0:T(8,128)(2,1)S(1)}, f32[2,64,1408]{2,1,0:...) custom-call(bf16[1,2,512,1408]{3,2,1,0:T(8,128)(2,1)} %refs_0_.1, ...), custom_call_target="tpu_custom_call" | custom-call | tf_op jit(solution)/shard_map/step/pallas_call | solution.py:290
  149.0 3.9 %flush.2 = (bf16[2,512,1408]{2,1,0:T(8,128)(2,1)}, bf16[2,512,1408]{2,1,0:T(8,128)(2,1)}, f32[2,64,1408]{2,1,0:T(8,128)}, f32[2,64,1408]{2,1,0:T(8,128)}, f32[2,...) custom-call(bf16[2,512,1408]{2,1,0:T(8,128)(2,1)S(1)} %get-tuple-ele, ...), custom_call_target="tpu_custom_call" | custom-call | tf_op jit(solution)/shard_map/flush/pallas_call | solution.py:271
  152.9 21.3 %last.1.refs_0_ = bf16[2,1408,512]{2,1,0:T(8,128)(2,1)S(1)} custom-call(bf16[2,176,512]{2,1,0:T(8,128)(2,1)S(1)} %get-tuple-element.37.own, f32[8,128]{1,0:T(8,128)S(1)} %get-tuple-element.38.token), custom_call_target="tpu_custom_call" | custom-call | tf_op jit(solution)/shard_map/last/pallas_call | solution.py:314
  174.2 1.6 flush.3

commit v4 on v3

--- a/solution.py
+++ b/solution.py
@@ -9,7 +9,8 @@
 
 MESH = pl.DeviceIdType.MESH
 TILE = 16
-LATER = 13500
+PIECES = 2
+LATER = 9500
 
 
 def adamw(w, m, v, g):
@@ -19,6 +20,10 @@
     return (w - 0.02 * step).astype(jnp.bfloat16), m, v
 
 
+def all_of_it(ref, sem):
+    pltpu.make_async_copy(ref, ref, sem).wait()
+
+
 class Gather:
     def __init__(self, n, towards, layers, hops, send_sem, recv_sem):
         self.n, self.towards, self.layers, self.hops = n, towards, layers, hops
@@ -33,30 +38,27 @@
         return pltpu.make_async_remote_copy(
             src_ref=to if source is None else source,
             dst_ref=to,
-            send_sem=self.send_sem.at[way, short, p],
+            send_sem=self.send_sem.at[way, p],
             recv_sem=self.recv_sem.at[way, 2 * s + short, p],
             device_id={"dp": self.towards[way]},
             device_id_type=MESH,
         )
 
-    def forward(self, pieces, own=None):
+    def forward(self, pieces, order):
         for s in range(self.hops[0]):
-            for p, (ref, *piece) in enumerate(pieces):
-                rows, start, size = piece
-                for short in range(2):
-                    for way in range(2):
-                        if s >= self.hops[short]:
-                            continue
-
-                        def copy(step, behind, source=None):
-                            return self.copy(ref, way, short, step, p, self.behind(way, behind), rows, start, size, source)
-
-                        with jax.named_scope(f"get{s}{p}{short}{way}"):
-                            copy(s, s + 1).wait_recv()
-                        mine = own.at[self.layers[way][short], pl.ds(start, size)] if own is not None and s == 0 else None
-                        copy(s, s, mine).wait_send()
-                        if s + 1 < self.hops[short]:
-                            copy(s + 1, s + 1).start()
+            for p, short in order:
+                ref, rows, start, size = pieces[p]
+                for way in range(2):
+                    if s >= self.hops[short]:
+                        continue
+
+                    def copy(step, behind):
+                        return self.copy(ref, way, short, step, p, self.behind(way, behind), rows, start, size)
+
+                    with jax.named_scope(f"get{s}{p}{short}{way}"):
+                        copy(s, s + 1).wait_recv()
+                    if s + 1 < self.hops[short]:
+                        copy(s + 1, s + 1).start()
 
 
 def kernel(n, count, *refs):
@@ -97,15 +99,13 @@
             [(weights[k].at[:, pl.ds(pl.multiple_of(me * rows[k], rows[k]), rows[k])], own[k]), (m_in[k], m_own[k]), (v_in[k], v_own[k])]
         )
     ]
-    for way in range(2):
-        first(way, 0, 0, 3).start()
     pl.semaphore_wait(barrier, 2)
     for k in range(3):
         for short in range(k == 0, 2):
             for way in range(2):
                 first(way, short, k, k).start()
 
-    @pl.when(lax.rem(lax.axis_index("rep"), 2) == 1)
+    @pl.when(lax.rem(lax.axis_index("rep"), 2) == 0)
     def _():
         pl.delay(LATER)
 
@@ -113,7 +113,7 @@
         return pltpu.make_async_remote_copy(
             src_ref=source,
             dst_ref=to,
-            send_sem=send_sem.at[way, short, k],
+            send_sem=send_sem.at[way, k],
             recv_sem=recv_sem.at[way, 2 * s + short, k],
             device_id={"dp": towards[way]},
             device_id_type=MESH,
@@ -121,14 +121,16 @@
 
     def sum_copy(way, short, s, k):
         source = raw[k].at[way, short] if s == 0 else came[k].at[way, 2 * (s - 1) + short]
+        if s == k == short == 0:
+            source = block(terms[k].at[0], layers[way][short], at(sign(way, hops[short])), k)
         return send(way, short, s, k, source, came[k].at[way, 2 * s + short])
 
     with jax.named_scope("first"):
         for k in range(3):
             for short in range(2):
-                if k == 0 or not short:
+                if short if k == 0 else not short:
                     ready = raw[k] if k else raw[k].at[:, short]
-                    pltpu.make_async_copy(ready, ready, load_sem.at[0 if short else (3, 1, 2)[k]]).wait()
+                    all_of_it(ready, load_sem.at[0 if short else (3, 1, 2)[k]])
                 for way in range(2):
                     sum_copy(way, short, 0, k).start()
             rest[k].start()
@@ -159,7 +161,6 @@
                             tile = pl.ds(pl.multiple_of(t * TILE, TILE), TILE)
                             mine[tile] = (mine[tile].astype(jnp.float32) + term[tile].astype(jnp.float32)).astype(jnp.bfloat16)
 
-                        sum_copy(way, short, s, k).wait_send()
                         sum_copy(way, short, s + 1, k).start()
                     elif not short:
                         other, to = came[k].at[1 - way, 2 * (s - 1) + 1], total[k].at[layer]
@@ -196,12 +197,11 @@
         for copy in owns:
             copy.wait()
         for way in range(2):
-            for short in range(2):
-                for k in range(3):
-                    sum_copy(way, short, hops[short] - 1, k).wait_send()
+            for k in range(3):
+                all_of_it(came[k].at[way], send_sem.at[way, k])
         others = parts.at[pl.ds(0, n - 1)]
         for i in range(2):
-            pltpu.make_async_copy(others, others, part_sem.at[i]).wait()
+            all_of_it(others, part_sem.at[i])
     factor = jnp.minimum(1.0, 0.5 * lax.rsqrt(jnp.sum(parts[...], keepdims=True) / count + 1e-30))
 
     gather = Gather(n, towards, layers, hops, send_sem, recv_sem)
@@ -224,7 +224,10 @@
             if k < last:
                 for way in range(2):
                     gather.copy(w_out[k], way, int(layer != way), 0, k, me, rows[k]).start()
-    gather.forward([(w_out[k], rows[k], 0, rows[k]) for k in range(last)])
+    gather.forward([(w_out[k], rows[k], 0, rows[k]) for k in range(last)], [(k, short) for k in range(last) for short in range(2)])
+    for way in range(2):
+        for k in range(last):
+            all_of_it(came[k].at[way], send_sem.at[way, k])
 
 
 def kernel_of_the_last(n, own, token, out, send_sem, recv_sem):
@@ -232,8 +235,9 @@
     me = lax.axis_index("dp")
     towards = (lax.rem(me + 1, n), lax.rem(me + n - 1, n))
     rows = own.shape[1]
-    cut = rows // 2 // TILE * TILE
-    cuts = [(0, rows - cut), (rows - cut, cut)]
+    edges = [rows // TILE * p // PIECES * TILE for p in range(PIECES + 1)]
+    cuts = [(start, end - start) for start, end in zip(edges, edges[1:])]
+    order = [(p, short) for short in range(2) for p in range(PIECES)]
     barrier = pltpu.get_barrier_semaphore()
     for peer in towards:
         pl.semaphore_signal(barrier, inc=1, device_id={"dp": peer}, device_id_type=MESH)
@@ -247,12 +251,15 @@
 
     pl.semaphore_wait(barrier, 2)
     gather = Gather(n, towards, [[way, 1 - way] for way in range(2)], [n // 2, n // 2 - 1], send_sem, recv_sem)
-    for p, (start, size) in enumerate(cuts):
-        for short in range(2):
-            for way in range(2):
-                source = own.at[gather.layers[way][short], pl.ds(start, size)]
-                gather.copy(out, way, short, 0, p, me, rows, start, size, source).start()
-    gather.forward([(out, rows, *cut) for cut in cuts], own)
+    for p, short in order:
+        start, size = cuts[p]
+        for way in range(2):
+            source = own.at[gather.layers[way][short], pl.ds(start, size)]
+            gather.copy(out, way, short, 0, p, me, rows, start, size, source).start()
+    gather.forward([(out, rows, *cut) for cut in cuts], order)
+    for way in range(2):
+        for p, (_, size) in enumerate(cuts):
+            all_of_it(out.at[0, pl.ds(0, sum(gather.hops) * size)], send_sem.at[way, p])
 
 
 def flush(count, *refs):
@@ -303,7 +310,7 @@
                 pltpu.VMEM((n, 128), jnp.float32),
                 pltpu.SemaphoreType.DMA((4,)),
                 pltpu.SemaphoreType.DMA((3, 3)),
-                pltpu.SemaphoreType.DMA((2, 2, 3)),
+                pltpu.SemaphoreType.DMA((2, 3)),
                 pltpu.SemaphoreType.DMA((2, 2 * half - 1, 3)),
                 pltpu.SemaphoreType.DMA((2,)),
             ],
@@ -317,7 +324,7 @@
             out_shape=pltpu.VMEM(weights[-1].shape, weights[-1].dtype),
             in_specs=[pl.BlockSpec(memory_space=pltpu.VMEM)] * 2,
             out_specs=pl.BlockSpec(memory_space=pltpu.VMEM),
-            scratch_shapes=[pltpu.SemaphoreType.DMA((2, 2, 2)), pltpu.SemaphoreType.DMA((2, 2 * half - 1, 2))],
+            scratch_shapes=[pltpu.SemaphoreType.DMA((2, PIECES)), pltpu.SemaphoreType.DMA((2, 2 * half - 1, PIECES))],
             compiler_params=pltpu.CompilerParams(collective_id=1, has_side_effects=True, vmem_limit_bytes=2**20),
         )(own, token)
         return (*done[: len(whole)], *flushed([last]), *done[len(whole) :])

time: 176 us -> 174 us (0.989)
  the two profiles are of different devices: /device:TPU:21 before, /device:TPU:22 now
where the time goes in v4:
time: 174 us
  Pallas kernels  173 us (99%)
    pallas_call x1, Pallas kernels, step(): pl.pallas_call(functools.partial(kernel, n, count), name='step', out_shap...  148 us
    pallas_call x1, Pallas kernels, step(): pl.pallas_call(functools.partial(kernel_of_the_last, n), name='last', out...  19.9 us
    pallas_call x2, Pallas kernels, flushed(): pl.pallas_call(functools.partial(flush, count), name='flush', out_shape=[...  5.5 us

profile of v4, /device:TPU:22, one launch (start us, length us, event | category | flops | bytes accessed | tf_op | source)
XLA Modules:
  0.0 173.7 jit_solution(17354851571855640143)
XLA Ops:
  0.6 147.7 %step.1 = (bf16[2,512,1408]{2,1,0:T(8,128)(2,1)S(1)}, bf16[2,512,1408]{2,1,0:T(8,128)(2,1)S(1)}, bf16[2,176,512]{2,1,0:T(8,128)(2,1)S(1)}, f32[2,64,1408]{2,1,0:...) custom-call(bf16[1,2,512,1408]{3,2,1,0:T(8,128)(2,1)} %refs_0_.1, ...), custom_call_target="tpu_custom_call" | custom-call | tf_op jit(solution)/shard_map/step/pallas_call | solution.py:297
  148.3 3.9 %flush.2 = (bf16[2,512,1408]{2,1,0:T(8,128)(2,1)}, bf16[2,512,1408]{2,1,0:T(8,128)(2,1)}, f32[2,64,1408]{2,1,0:T(8,128)}, f32[2,64,1408]{2,1,0:T(8,128)}, f32[2,...) custom-call(bf16[2,512,1408]{2,1,0:T(8,128)(2,1)S(1)} %get-tuple-ele, ...), custom_call_target="tpu_custom_call" | custom-call | tf_op jit(solution)/shard_map/flush/pallas_call | solution.py:278
  152.3 19.9 %last.1.refs_0_ = bf16[2,1408,512]{2,1,0:T(8,128)(2,1)S(1)} custom-call(bf16[2,176,512]{2,1,0:T(8,128)(2,1)S(1)} %get-tuple-element.37.own, f32[8,128]{1,0:T(8,128)S(1)} %get-tuple-element.38.token), custom_call_target="tpu_custom_call" | custom-call | tf_op jit(solution)/shard_map/last/pallas_call | solution.py:321
  172.1 1.6 flush.3

commit v5 on v4

--- a/solution.py
+++ b/solution.py
@@ -55,8 +55,7 @@
                     def copy(step, behind):
                         return self.copy(ref, way, short, step, p, self.behind(way, behind), rows, start, size)
 
-                    with jax.named_scope(f"get{s}{p}{short}{way}"):
-                        copy(s, s + 1).wait_recv()
+                    copy(s, s + 1).wait_recv()
                     if s + 1 < self.hops[short]:
                         copy(s + 1, s + 1).start()
 
@@ -87,9 +86,8 @@
     for peer in towards:
         pl.semaphore_signal(barrier, inc=1, device_id={"dp": peer}, device_id_type=MESH)
 
-    def first(way, short, k, sem):
-        source = block(terms[k].at[0], layers[way][short], at(sign(way, hops[short])), k)
-        return pltpu.make_async_copy(source, raw[k].at[way, short], load_sem.at[sem])
+    def begins(way, short, k):
+        return block(terms[k].at[0], layers[way][short], at(sign(way, hops[short])), k)
 
     rest = [pltpu.make_async_copy(terms[k].at[0], held[k], load_sem.at[k]) for k in range(3)]
     owns = [
@@ -103,7 +101,7 @@
     for k in range(3):
         for short in range(k == 0, 2):
             for way in range(2):
-                first(way, short, k, k).start()
+                pltpu.make_async_copy(begins(way, short, k), raw[k].at[way, short], load_sem.at[k]).start()
 
     @pl.when(lax.rem(lax.axis_index("rep"), 2) == 0)
     def _():
@@ -120,22 +118,22 @@
         )
 
     def sum_copy(way, short, s, k):
-        source = raw[k].at[way, short] if s == 0 else came[k].at[way, 2 * (s - 1) + short]
-        if s == k == short == 0:
-            source = block(terms[k].at[0], layers[way][short], at(sign(way, hops[short])), k)
+        if s:
+            source = came[k].at[way, 2 * (s - 1) + short]
+        else:
+            source = raw[k].at[way, short] if k or short else begins(way, short, k)
         return send(way, short, s, k, source, came[k].at[way, 2 * s + short])
 
-    with jax.named_scope("first"):
-        for k in range(3):
-            for short in range(2):
-                if short if k == 0 else not short:
-                    ready = raw[k] if k else raw[k].at[:, short]
-                    all_of_it(ready, load_sem.at[0 if short else (3, 1, 2)[k]])
-                for way in range(2):
-                    sum_copy(way, short, 0, k).start()
-            rest[k].start()
-        for copy in owns:
-            copy.start()
+    for way in range(2):
+        sum_copy(way, 0, 0, 0).start()
+    for k in range(3):
+        all_of_it(raw[k] if k else raw[k].at[:, 1], load_sem.at[k])
+        for short in range(k == 0, 2):
+            for way in range(2):
+                sum_copy(way, short, 0, k).start()
+        rest[k].start()
+    for copy in owns:
+        copy.start()
 
     squares = jnp.zeros((8, 128), jnp.float32)
     waited = set()
@@ -148,8 +146,7 @@
                         continue
                     layer = layers[way][short]
                     mine = came[k].at[way, 2 * s + short]
-                    with jax.named_scope(f"recv{s}{k}{short}{way}"):
-                        sum_copy(way, short, s, k).wait_recv()
+                    sum_copy(way, short, s, k).wait_recv()
                     if k not in waited:
                         waited.add(k)
                         rest[k].wait()
@@ -190,18 +187,17 @@
             device_id_type=MESH,
         )
 
-    with jax.named_scope("exchange"):
-        parts[pl.ds(me, 1)] = jnp.sum(squares, axis=0, keepdims=True)
-        for away in sorted(range(1, n), key=lambda away: -min(away, n - away)):
-            part_copy(away, me).start()
-        for copy in owns:
-            copy.wait()
-        for way in range(2):
-            for k in range(3):
-                all_of_it(came[k].at[way], send_sem.at[way, k])
-        others = parts.at[pl.ds(0, n - 1)]
-        for i in range(2):
-            all_of_it(others, part_sem.at[i])
+    parts[pl.ds(me, 1)] = jnp.sum(squares, axis=0, keepdims=True)
+    for away in sorted(range(1, n), key=lambda away: -min(away, n - away)):
+        part_copy(away, me).start()
+    for copy in owns:
+        copy.wait()
+    for way in range(2):
+        for k in range(3):
+            all_of_it(came[k].at[way], send_sem.at[way, k])
+    others = parts.at[pl.ds(0, n - 1)]
+    for i in range(2):
+        all_of_it(others, part_sem.at[i])
     factor = jnp.minimum(1.0, 0.5 * lax.rsqrt(jnp.sum(parts[...], keepdims=True) / count + 1e-30))
 
     gather = Gather(n, towards, layers, hops, send_sem, recv_sem)
@@ -210,16 +206,15 @@
         for layer in range(2):
             to = w_out[k].at[layer] if k == last else block(w_out[k], layer, me, k)
 
-            with jax.named_scope(f"adamw{k}{layer}"):
-
-                @pl.loop(0, rows[k] // TILE)
-                def _(t):
-                    tile = pl.ds(pl.multiple_of(t * TILE, TILE), TILE)
-                    g = total[k][layer, tile].astype(jnp.float32) * factor
-                    w, m, v = adamw(own[k][layer, tile].astype(jnp.float32), m_own[k][layer, tile], v_own[k][layer, tile], g)
-                    to[tile] = w
-                    m_out[k][layer, tile] = m
-                    v_out[k][layer, tile] = v
+
+            @pl.loop(0, rows[k] // TILE)
+            def _(t):
+                tile = pl.ds(pl.multiple_of(t * TILE, TILE), TILE)
+                g = total[k][layer, tile].astype(jnp.float32) * factor
+                w, m, v = adamw(own[k][layer, tile].astype(jnp.float32), m_own[k][layer, tile], v_own[k][layer, tile], g)
+                to[tile] = w
+                m_out[k][layer, tile] = m
+                v_out[k][layer, tile] = v
 
             if k < last:
                 for way in range(2):
@@ -308,7 +303,7 @@
                 *(pltpu.VMEM((2, *b), jnp.float32) for b in blocks * 2),
                 *(pltpu.VMEM((2, *b), jnp.bfloat16) for b in blocks),
                 pltpu.VMEM((n, 128), jnp.float32),
-                pltpu.SemaphoreType.DMA((4,)),
+                pltpu.SemaphoreType.DMA((3,)),
                 pltpu.SemaphoreType.DMA((3, 3)),
                 pltpu.SemaphoreType.DMA((2, 3)),
                 pltpu.SemaphoreType.DMA((2, 2 * half - 1, 3)),

time: 174 us -> 174 us (level)
  no operation moved by 1% of the time
where the time goes in v5:
time: 174 us
  Pallas kernels  173 us (99%)
    pallas_call x1, Pallas kernels, step(): pl.pallas_call(functools.partial(kernel, n, count), name='step', out_shap...  148 us
    pallas_call x1, Pallas kernels, step(): pl.pallas_call(functools.partial(kernel_of_the_last, n), name='last', out...  19.9 us
    pallas_call x2, Pallas kernels, flushed(): pl.pallas_call(functools.partial(flush, count), name='flush', out_shape=[...  5.5 us

profile of v5, /device:TPU:22, one launch (start us, length us, event | category | flops | bytes accessed | tf_op | source)
XLA Modules:
  0.0 173.7 jit_solution(11935805947714604956)
XLA Ops:
  0.6 147.7 %step.1 = (bf16[2,512,1408]{2,1,0:T(8,128)(2,1)S(1)}, bf16[2,512,1408]{2,1,0:T(8,128)(2,1)S(1)}, bf16[2,176,512]{2,1,0:T(8,128)(2,1)S(1)}, f32[2,64,1408]{2,1,0:...) custom-call(bf16[1,2,512,1408]{3,2,1,0:T(8,128)(2,1)} %refs_0_.1, ...), custom_call_target="tpu_custom_call" | custom-call | tf_op jit(solution)/shard_map/step/pallas_call | solution.py:292
  148.3 3.9 %flush.2 = (bf16[2,512,1408]{2,1,0:T(8,128)(2,1)}, bf16[2,512,1408]{2,1,0:T(8,128)(2,1)}, f32[2,64,1408]{2,1,0:T(8,128)}, f32[2,64,1408]{2,1,0:T(8,128)}, f32[2,...) custom-call(bf16[2,512,1408]{2,1,0:T(8,128)(2,1)S(1)} %get-tuple-ele, ...), custom_call_target="tpu_custom_call" | custom-call | tf_op jit(solution)/shard_map/flush/pallas_call | solution.py:273
  152.3 19.9 %last.1.refs_0_ = bf16[2,1408,512]{2,1,0:T(8,128)(2,1)S(1)} custom-call(bf16[2,176,512]{2,1,0:T(8,128)(2,1)S(1)} %get-tuple-element.37.own, f32[8,128]{1,0:T(8,128)S(1)} %get-tuple-element.38.token), custom_call_target="tpu_custom_call" | custom-call | tf_op jit(solution)/shard_map/last/pallas_call | solution.py:316
  172.1 1.6 flush.3

commit v6 on v5

--- a/solution.py
+++ b/solution.py
@@ -225,17 +225,35 @@
             all_of_it(came[k].at[way], send_sem.at[way, k])
 
 
-def kernel_of_the_last(n, own, token, out, send_sem, recv_sem):
+def kernel_of_the_last(n, own, token, out, send_sem, recv_sem, end_sem):
     del token
     me = lax.axis_index("dp")
     towards = (lax.rem(me + 1, n), lax.rem(me + n - 1, n))
-    rows = own.shape[1]
-    edges = [rows // TILE * p // PIECES * TILE for p in range(PIECES + 1)]
-    cuts = [(start, end - start) for start, end in zip(edges, edges[1:])]
-    order = [(p, short) for short in range(2) for p in range(PIECES)]
     barrier = pltpu.get_barrier_semaphore()
     for peer in towards:
         pl.semaphore_signal(barrier, inc=1, device_id={"dp": peer}, device_id_type=MESH)
+    rows = own.shape[1]
+    hops = [n // 2, n // 2 - 1]
+    edges = [rows // TILE * p // PIECES * TILE for p in range(PIECES + 1)]
+    order = [(p, short) for short in range(2) for p in range(PIECES)]
+
+    def copy(way, short, s, p, behind):
+        layer, start, size = way if not short else 1 - way, edges[p], edges[p + 1] - edges[p]
+        sender = lax.rem(me + (-behind if way == 0 else behind) + n, n)
+        to = out.at[layer, pl.ds(pl.multiple_of(sender * rows + start, TILE), size)]
+        return pltpu.make_async_remote_copy(
+            src_ref=to if s else own.at[layer, pl.ds(start, size)],
+            dst_ref=to,
+            send_sem=send_sem.at[way],
+            recv_sem=end_sem.at[way] if s == hops[short] - 1 else recv_sem.at[way, 2 * s + short, p],
+            device_id={"dp": towards[way]},
+            device_id_type=MESH,
+        )
+
+    pl.semaphore_wait(barrier, 2)
+    for p, short in order:
+        for way in range(2):
+            copy(way, short, 0, p, 0).start()
     first = pl.multiple_of(me * rows, rows)
 
     @pl.loop(0, rows // TILE)
@@ -244,17 +262,15 @@
         for layer in range(2):
             out[layer, pl.ds(pl.multiple_of(first + tile, TILE), TILE)] = own[layer, pl.ds(tile, TILE)]
 
-    pl.semaphore_wait(barrier, 2)
-    gather = Gather(n, towards, [[way, 1 - way] for way in range(2)], [n // 2, n // 2 - 1], send_sem, recv_sem)
-    for p, short in order:
-        start, size = cuts[p]
-        for way in range(2):
-            source = own.at[gather.layers[way][short], pl.ds(start, size)]
-            gather.copy(out, way, short, 0, p, me, rows, start, size, source).start()
-    gather.forward([(out, rows, *cut) for cut in cuts], order)
+    for s in range(hops[0] - 1):
+        for p, short in order:
+            for way in range(2):
+                if s < hops[short] - 1:
+                    copy(way, short, s, p, s + 1).wait_recv()
+                    copy(way, short, s + 1, p, s + 1).start()
     for way in range(2):
-        for p, (_, size) in enumerate(cuts):
-            all_of_it(out.at[0, pl.ds(0, sum(gather.hops) * size)], send_sem.at[way, p])
+        all_of_it(own, end_sem.at[way])
+        all_of_it(out.at[0, pl.ds(0, sum(hops) * rows)], send_sem.at[way])
 
 
 def flush(count, *refs):
@@ -319,7 +335,11 @@
             out_shape=pltpu.VMEM(weights[-1].shape, weights[-1].dtype),
             in_specs=[pl.BlockSpec(memory_space=pltpu.VMEM)] * 2,
             out_specs=pl.BlockSpec(memory_space=pltpu.VMEM),
-            scratch_shapes=[pltpu.SemaphoreType.DMA((2, PIECES)), pltpu.SemaphoreType.DMA((2, 2 * half - 1, PIECES))],
+            scratch_shapes=[
+                pltpu.SemaphoreType.DMA((2,)),
+                pltpu.SemaphoreType.DMA((2, 2 * half - 3, PIECES)),
+                pltpu.SemaphoreType.DMA((2,)),
+            ],
             compiler_params=pltpu.CompilerParams(collective_id=1, has_side_effects=True, vmem_limit_bytes=2**20),
         )(own, token)
         return (*done[: len(whole)], *flushed([last]), *done[len(whole) :])

time: 174 us -> 174 us (level)
  no operation moved by 1% of the time
where the time goes in v6:
time: 174 us
  Pallas kernels  173 us (99%)
    pallas_call x1, Pallas kernels, step(): pl.pallas_call(functools.partial(kernel, n, count), name='step', out_shap...  148 us
    pallas_call x1, Pallas kernels, step(): pl.pallas_call(functools.partial(kernel_of_the_last, n), name='last', out...  19.7 us
    pallas_call x2, Pallas kernels, flushed(): pl.pallas_call(functools.partial(flush, count), name='flush', out_shape=[...  5.5 us

profile of v6, /device:TPU:22, one launch (start us, length us, event | category | flops | bytes accessed | tf_op | source)
XLA Modules:
  0.0 173.6 jit_solution(6911790850911692330)
XLA Ops:
  0.6 147.8 %step.1 = (bf16[2,512,1408]{2,1,0:T(8,128)(2,1)S(1)}, bf16[2,512,1408]{2,1,0:T(8,128)(2,1)S(1)}, bf16[2,176,512]{2,1,0:T(8,128)(2,1)S(1)}, f32[2,64,1408]{2,1,0:...) custom-call(bf16[1,2,512,1408]{3,2,1,0:T(8,128)(2,1)} %refs_0_.1, ...), custom_call_target="tpu_custom_call" | custom-call | tf_op jit(solution)/shard_map/step/pallas_call | solution.py:308
  148.4 3.9 %flush.2 = (bf16[2,512,1408]{2,1,0:T(8,128)(2,1)}, bf16[2,512,1408]{2,1,0:T(8,128)(2,1)}, f32[2,64,1408]{2,1,0:T(8,128)}, f32[2,64,1408]{2,1,0:T(8,128)}, f32[2,...) custom-call(bf16[2,512,1408]{2,1,0:T(8,128)(2,1)S(1)} %get-tuple-ele, ...), custom_call_target="tpu_custom_call" | custom-call | tf_op jit(solution)/shard_map/flush/pallas_call | solution.py:289
  152.3 19.7 %last.1.refs_0_ = bf16[2,1408,512]{2,1,0:T(8,128)(2,1)S(1)} custom-call(bf16[2,176,512]{2,1,0:T(8,128)(2,1)S(1)} %get-tuple-element.37.own, f32[8,128]{1,0:T(8,128)S(1)} %get-tuple-element.38.token), custom_call_target="tpu_custom_call" | custom-call | tf_op jit(solution)/shard_map/last/pallas_call | solution.py:332
  172.1 1.6 flush.3

commit v7 on v6

--- a/solution.py
+++ b/solution.py
@@ -97,11 +97,11 @@
             [(weights[k].at[:, pl.ds(pl.multiple_of(me * rows[k], rows[k]), rows[k])], own[k]), (m_in[k], m_own[k]), (v_in[k], v_own[k])]
         )
     ]
-    pl.semaphore_wait(barrier, 2)
     for k in range(3):
         for short in range(k == 0, 2):
             for way in range(2):
                 pltpu.make_async_copy(begins(way, short, k), raw[k].at[way, short], load_sem.at[k]).start()
+    pl.semaphore_wait(barrier, 2)
 
     @pl.when(lax.rem(lax.axis_index("rep"), 2) == 0)
     def _():

time: 174 us -> 174 us (level)
  no operation moved by 1% of the time
where the time goes in v7:
time: 174 us
  Pallas kernels  173 us (99%)
    pallas_call x1, Pallas kernels, step(): pl.pallas_call(functools.partial(kernel, n, count), name='step', out_shap...  148 us
    pallas_call x1, Pallas kernels, step(): pl.pallas_call(functools.partial(kernel_of_the_last, n), name='last', out...  19.7 us
    pallas_call x2, Pallas kernels, flushed(): pl.pallas_call(functools.partial(flush, count), name='flush', out_shape=[...  5.5 us

profile of v7, /device:TPU:22, one launch (start us, length us, event | category | flops | bytes accessed | tf_op | source)
XLA Modules:
  0.0 173.6 jit_solution(10196935454489040432)
XLA Ops:
  0.6 147.8 %step.1 = (bf16[2,512,1408]{2,1,0:T(8,128)(2,1)S(1)}, bf16[2,512,1408]{2,1,0:T(8,128)(2,1)S(1)}, bf16[2,176,512]{2,1,0:T(8,128)(2,1)S(1)}, f32[2,64,1408]{2,1,0:...) custom-call(bf16[1,2,512,1408]{3,2,1,0:T(8,128)(2,1)} %refs_0_.1, ...), custom_call_target="tpu_custom_call" | custom-call | tf_op jit(solution)/shard_map/step/pallas_call | solution.py:308
  148.4 3.9 %flush.2 = (bf16[2,512,1408]{2,1,0:T(8,128)(2,1)}, bf16[2,512,1408]{2,1,0:T(8,128)(2,1)}, f32[2,64,1408]{2,1,0:T(8,128)}, f32[2,64,1408]{2,1,0:T(8,128)}, f32[2,...) custom-call(bf16[2,512,1408]{2,1,0:T(8,128)(2,1)S(1)} %get-tuple-ele, ...), custom_call_target="tpu_custom_call" | custom-call | tf_op jit(solution)/shard_map/flush/pallas_call | solution.py:289
  152.3 19.7 %last.1.refs_0_ = bf16[2,1408,512]{2,1,0:T(8,128)(2,1)S(1)} custom-call(bf16[2,176,512]{2,1,0:T(8,128)(2,1)S(1)} %get-tuple-element.37.own, f32[8,128]{1,0:T(8,128)S(1)} %get-tuple-element.38.token), custom_call_target="tpu_custom_call" | custom-call | tf_op jit(solution)/shard_map/last/pallas_call | solution.py:332
  172.0 1.6 flush.3
